TPU v7x, 32 devices: a whole 2x2x4 slice. The times are simulated.
32 devices in a mesh: pair: 8 (over y, x, core), aux: 4 (over z).
Axes of the slice: x: 2, y: 2, z: 4, core: 2. Of those that a mesh axis runs over, the one named last changes fastest.
Arguments:
- integrals: bfloat16 [512, 256, 64], P(('pair', 'aux')), may hold values from -6 to 6
- amplitudes: bfloat16 [512, 64, 64], P(('pair', 'aux')), may hold values from -0.75 to 0.75
- pno_density: bfloat16 [512, 64, 64], P(('pair', 'aux')), may hold values from -6 to 6
- pno_coef: bfloat16 [512, 256, 64], P(('pair', 'aux')), may hold values from -0.75 to 0.75
- pao_blocks: int32 [512, 2], P(('pair', 'aux')), may hold values from 0 to 5, all different within a row
- aux_slice: int32 [512, 2], P(('pair', 'aux')), may hold values from 0 to 3, all different within a row; in each aligned block of 16 rows (0 to 15, 16 to 31, ...) at most 16 rows name the same one
- aux_offset: int32 [512, 2], P(('pair', 'aux')), may hold values from 0 to 3
Outputs:
- aux_density: float32 [2048, 768], P('aux', 'pair')
- virtual_density: float32 [768, 768], P('aux', 'pair')
Inputs may be any that keep to these rules, and one draw needn't show every extreme that they name: `pao_blocks`: the 2 blocks of a pair are different. `aux_slice`: the 2 slices of a pair are different; among the pairs of one device no slice is named more than 16 times, and in every draw some device names some slice exactly 16 times.
All inputs are finite; a program needn't handle non-finite values.
Results may differ from a plain program's by a relative error of at most 0.0041.
Values may be sent and summed in bfloat16 or wider, within the bound.
A program may use at most 64 MiB of HBM per device.

v0:
```python
import functools
import math

import jax
import jax.numpy as jnp
from jax import lax
from jax.experimental import pallas as pl
from jax.experimental.pallas import tpu as pltpu
from jax.sharding import PartitionSpec as P

NBLK = 6
ABPO = 4
MESH = pl.DeviceIdType.MESH
TILE = 128
SUB = 16


def by_collectives(integrals, amplitudes, pno_density, pno_coef, pao_blocks, aux_slice, aux_offset):
    n_pair = lax.axis_size("pair")
    n_aux = lax.axis_size("aux")
    pair_count, domain_rows, pno_rank = pno_coef.shape
    aux_dom = aux_slice.shape[1]
    pao_dom = pao_blocks.shape[1]
    pao_block = domain_rows // pao_dom
    aux_block = integrals.shape[1] // aux_dom
    ao_count = NBLK * pao_block
    capacity = max(2, 2 * pair_count * aux_dom // n_aux)
    out_scale = 1.0 / math.sqrt(pair_count * n_pair)
    slot_count = pair_count * aux_dom
    three_index = jnp.einsum(
        "pqr,prs->pqs", integrals, amplitudes, preferred_element_type=jnp.float32
    ).astype(jnp.bfloat16)
    owners = aux_slice.reshape(slot_count)
    owner_hot = (owners[:, None] == jnp.arange(n_aux, dtype=jnp.int32)[None, :]).astype(jnp.int32)
    before = jnp.cumsum(owner_hot, 0) - owner_hot
    slot_rank = jnp.sum(before * owner_hot, 1)
    target = owners * capacity + slot_rank
    routing = jnp.arange(n_aux * capacity, dtype=jnp.int32)[:, None] == target[None, :]
    labels = (
        jnp.concatenate(
            [aux_offset.reshape(slot_count, 1), jnp.repeat(pao_blocks, aux_dom, axis=0)], 1
        )
        + 1
    )
    label_buffer = (jnp.dot(routing.astype(jnp.int32), labels) - 1).reshape(
        n_aux, capacity, 1 + pao_dom
    )
    routing_bf = routing.astype(jnp.bfloat16)
    index_flat = three_index.reshape(slot_count, aux_block * pno_rank)
    index_buffer = jnp.dot(routing_bf, index_flat, preferred_element_type=jnp.float32).astype(
        jnp.bfloat16
    )
    index_buffer = index_buffer.reshape(n_aux, capacity, aux_block, pno_rank)
    pair_routing = (
        routing.reshape(n_aux * capacity, pair_count, aux_dom).sum(-1).astype(jnp.bfloat16)
    )
    coef_flat = pno_coef.reshape(pair_count, domain_rows * pno_rank)
    coef_buffer = jnp.dot(pair_routing, coef_flat, preferred_element_type=jnp.float32).astype(
        jnp.bfloat16
    )
    coef_buffer = coef_buffer.reshape(n_aux, capacity, domain_rows, pno_rank)
    index_part = lax.all_to_all(index_buffer, "aux", split_axis=0, concat_axis=0, tiled=True)
    coef_part = lax.all_to_all(coef_buffer, "aux", split_axis=0, concat_axis=0, tiled=True)
    label_part = lax.all_to_all(label_buffer, "aux", split_axis=0, concat_axis=0, tiled=True)
    back = jnp.einsum(
        "ncxr,ncyr->ncxy", index_part, coef_part, preferred_element_type=jnp.float32
    ).astype(jnp.bfloat16)
    got_labels = label_part
    received_count = n_aux * capacity
    pieces = back.reshape(received_count, aux_block, pao_dom, pao_block)
    got_labels = got_labels.reshape(received_count, 1 + pao_dom)
    offset_hot = got_labels[:, 0:1] == jnp.arange(ABPO, dtype=jnp.int32)[None, :]
    column_hot = got_labels[:, 1:, None] == jnp.arange(NBLK, dtype=jnp.int32)[None, None, :]
    placement = (offset_hot[:, None, :, None] & column_hot[:, :, None, :]).astype(jnp.bfloat16)
    gamma_part = jnp.einsum(
        "sxhy,shok->oxky", pieces, placement, preferred_element_type=jnp.float32
    )
    gamma_part = gamma_part.reshape(ABPO * aux_block, ao_count)
    aux_density = lax.psum_scatter(gamma_part, "pair", scatter_dimension=1, tiled=True) * out_scale
    weighted = jnp.einsum(
        "pyr,prs->pys", pno_coef, pno_density, preferred_element_type=jnp.float32
    ).astype(jnp.bfloat16)
    block_hot = (pao_blocks[:, :, None] == jnp.arange(NBLK, dtype=jnp.int32)[None, None, :]).astype(
        jnp.bfloat16
    )
    weighted_rows = jnp.einsum(
        "pak,paxr->kxpr",
        block_hot,
        weighted.reshape(pair_count, pao_dom, pao_block, pno_rank),
        preferred_element_type=jnp.float32,
    ).astype(jnp.bfloat16)
    weighted_rows = weighted_rows.reshape(ao_count, pair_count * pno_rank)
    coef_rows = jnp.einsum(
        "pak,paxr->kxpr",
        block_hot,
        pno_coef.reshape(pair_count, pao_dom, pao_block, pno_rank),
        preferred_element_type=jnp.float32,
    ).astype(jnp.bfloat16)
    coef_rows = coef_rows.reshape(ao_count, pair_count * pno_rank)
    virt_part = lax.dot_general(
        weighted_rows, coef_rows, (((1,), (1,)), ((), ())), preferred_element_type=jnp.float32
    )
    row_owned = lax.psum_scatter(virt_part, "aux", scatter_dimension=0, tiled=True)
    virtual_density = lax.psum_scatter(row_owned, "pair", scatter_dimension=1, tiled=True)
    return (aux_density, virtual_density * out_scale)


def group_rows(shard):
    units = shard // SUB
    c = max(1, units // 6)
    a = units // 2
    return a * SUB, (units - a - c) * SUB, c * SUB


def kernel(scale, ints, amps, dens, coef, pao, aux, off, gamma, virt, out, coef2, tri2, wei2, ids, lhs, rhs, own, c_send, c_recv,
           ax_send, ax_recv, ay_send, ay_recv, by_send, by_recv, bx_send, bx_recv, keep1, keep2, cz_send, cz_recv,
           cw_send, cw_recv, ck, pz_send, pz_recv, pw_send, pw_recv, cx_send, cx_recv, cy_send, cy_recv, ckx, turned,
           send_sems, recv_sems):
    pairs, rank, rows = coef.shape
    couples = pairs // 2
    shard = gamma.shape[0]
    na, nb, nc = group_rows(shard)
    nab = na + nb
    lanes = out.shape[1]
    p = lax.axis_index("pair")
    z = lax.axis_index("aux")
    c, x, y = p % 2, (p // 2) % 2, p // 4
    z0, z1 = z % 2, z // 2
    core = (p + 1 - 2 * c, z)
    xdev = (p + 2 - 4 * x, z)
    ydev = (p + 4 - 8 * y, z)
    z0dev = (p, z + 1 - 2 * z0)
    z1dev = (p, z + 2 - 4 * z1)

    barrier = pltpu.get_barrier_semaphore()
    for dev in (core, xdev, ydev, z0dev, z1dev):
        pl.semaphore_signal(barrier, inc=1, device_id=dev, device_id_type=MESH)

    started = []

    def send(src, dst, dev):
        n = len(started)
        copy = pltpu.make_async_remote_copy(
            src_ref=src, dst_ref=dst, send_sem=send_sems.at[n], recv_sem=recv_sems.at[n],
            device_id=dev, device_id_type=MESH)
        copy.start()
        started.append(copy)
        return copy

    low = lax.broadcasted_iota(jnp.int32, (SUB, TILE), 1) < rank
    for q in range(couples):
        at = slice(q * TILE, (q + 1) * TILE)
        for h in range(2):
            ids[h, :, at] = jnp.where(low, pao[h, 2 * q], pao[h, 2 * q + 1])

    zero = jnp.zeros((rank, rank), jnp.bfloat16)

    def mixed(ref, q, both):
        diag = jnp.concatenate(
            [jnp.concatenate([ref[2 * q], zero], 1), jnp.concatenate([zero, ref[2 * q + 1]], 1)], 0)
        return lax.dot_general(
            diag, both, (((0,), (0,)), ((), ())), preferred_element_type=jnp.float32).astype(jnp.bfloat16)

    for q in range(couples):
        at = slice(q * TILE, (q + 1) * TILE)
        both = coef[2 * q:2 * q + 2].reshape(2 * rank, rows)
        coef2[:, at] = both.T
        wei2[at, :] = mixed(dens, q, both)
        tri2[at, :] = mixed(amps, q, ints[2 * q:2 * q + 2].reshape(2 * rank, rows))

    def mask(row, value):
        return jnp.where(ids[row] == value, 1.0, 0.0).astype(jnp.bfloat16)

    half_rows = rows // 2

    def place(dst, dst_row, src, src_row, count, first, value):
        m0, m1 = mask(first, value), mask(first + 1, value)
        for r in range(0, count, SUB):
            a = src[pl.ds(pl.multiple_of(src_row + r, SUB), SUB), :]
            b = src[pl.ds(pl.multiple_of(src_row + half_rows + r, SUB), SUB), :]
            dst[pl.ds(pl.multiple_of(dst_row + r, SUB), SUB), :] = a * m0 + b * m1

    for count, base, offset, y_first in ((na, 0, 0, 0), (nb, 4 * na, na, 1), (nc, 4 * nab, nab, 0)):

        def lhs_unit(n, carry, count=count, base=base, offset=offset, y_first=y_first):
            pieces = count // SUB
            half, ij, t = n // (4 * pieces), (n // pieces) % 4, n % pieces
            i, j = ij // 2, ij % 2
            si, sj = (j, i) if y_first else (i, j)
            cc = (1 - half) * (1 - c) + half * c
            xx = (1 - si) * (1 - x) + si * x
            yy = (1 - sj) * (1 - y) + sj * y
            row = ((yy * 2 + xx) * 2 + cc) * shard + offset + t * SUB
            place(lhs, half * (4 * shard) + base + (ij * pieces + t) * SUB, coef2,
                  row % half_rows, SUB, 0, row // half_rows)
            return carry

        lax.fori_loop(0, 8 * (count // SUB), lhs_unit, 0)

    chunk_of = ((1 - z1) * 2 + 1 - z0, (1 - z1) * 2 + z0, z1 * 2 + 1 - z0, z)

    def build(step):
        k = chunk_of[step]
        virt_first = 3 * (k // 2) + k % 2

        def switch(label, value):
            return jnp.full((rank, TILE), jnp.where(label == value, 1.0, 0.0), jnp.float32).astype(jnp.bfloat16)

        def one_pair(n, carry):
            at = pl.ds(pl.multiple_of(n * rank, rank), rank)
            for src, blocks, labels, start, base in (
                (tri2, ABPO, [aux[h, n] * ABPO + off[h, n] for h in range(2)], k * ABPO, 0),
                (wei2, 2, [pao[h, n] for h in range(2)], virt_first, ABPO),
            ):
                low_part, high_part = src[at, 0:TILE], src[at, TILE:2 * TILE]
                for j in range(blocks):
                    rhs[step % 2, at, (base + j) * TILE:(base + j + 1) * TILE] = (
                        low_part * switch(labels[0], start + j) + high_part * switch(labels[1], start + j))
            return carry

        lax.fori_loop(0, pairs, one_pair, 0, unroll=2)

    n_rows = 4 * shard
    wide = 2 * TILE

    def product(step, half, dst, kind):
        left = lhs.at[pl.ds(half * n_rows, n_rows)]

        def body(t, carry):
            at = pl.ds(pl.multiple_of(t * wide, wide), wide)
            dst[:, at] = lax.dot_general(
                left[...], rhs[step % 2, :, at], (((1,), (0,)), ((), ())),
                preferred_element_type=jnp.float32).astype(kind)
            return carry

        lax.fori_loop(0, lanes // wide, body, 0)

    f32, bf16 = jnp.float32, jnp.bfloat16
    stage1 = {}
    stage2 = {}
    zcopy = {}
    to_b, to_c = 4 * na, 4 * nab
    a_dev, b_dev = (xdev, ydev), (ydev, xdev)

    def first(step):
        stage1[step, "c"].wait_recv()

        def summed(lo, hi):
            return own[lo:hi, :] + c_recv[step, lo:hi, :].astype(f32)

        def quarters(base, count):
            order = (0, 1, 2, 3) if step % 2 == 0 else (0, 2, 1, 3)
            return [summed(base + n * count, base + (n + 1) * count) for n in order]

        a_parts, b_parts = quarters(0, na), quarters(to_b, nb)
        ax_send[step, 0:na] = a_parts[0].astype(bf16)
        ax_send[step, na:2 * na] = a_parts[1].astype(bf16)
        stage1[step, "a"] = send(ax_send.at[step], ax_recv.at[step], a_dev[step % 2])
        by_send[step, 0:nb] = b_parts[0].astype(bf16)
        by_send[step, nb:2 * nb] = b_parts[1].astype(bf16)
        stage1[step, "b"] = send(by_send.at[step], by_recv.at[step], b_dev[step % 2])
        if step in (0, 2):
            cz_send[step // 2] = summed(to_c, to_c + 4 * nc).astype(bf16)
            zcopy["c", step] = send(cz_send.at[step // 2], cz_recv.at[step // 2], z0dev)
        else:
            ck[step // 2] = summed(to_c, to_c + 4 * nc)
        mid = 2 * na
        keep1[step, 0:na] = a_parts[2]
        keep1[step, na:mid] = a_parts[3]
        keep1[step, mid:mid + nb] = b_parts[2]
        keep1[step, mid + nb:2 * nab] = b_parts[3]

    def second(step):
        stage1[step, "a"].wait_recv()
        ay_send[step] = (keep1[step, 0:na] + ax_recv[step, 0:na].astype(f32)).astype(bf16)
        stage2[step, "a"] = send(ay_send.at[step], ay_recv.at[step], b_dev[step % 2])
        stage1[step, "b"].wait_recv()
        mid = 2 * na
        bx_send[step] = (keep1[step, mid:mid + nb] + by_recv[step, 0:nb].astype(f32)).astype(bf16)
        stage2[step, "b"] = send(bx_send.at[step], bx_recv.at[step], a_dev[step % 2])
        keep2[step, 0:na] = keep1[step, na:mid] + ax_recv[step, na:mid].astype(f32)
        keep2[step, na:nab] = keep1[step, mid + nb:2 * nab] + by_recv[step, nb:2 * nb].astype(f32)

    def third_sum(step, lo, hi):
        got = ay_recv if lo == 0 else bx_recv
        return keep2[step, lo:hi] + got[step].astype(f32)

    halves = ((0, na), (na, nab))

    def third(step):
        stage2[step, "a"].wait_recv()
        stage2[step, "b"].wait_recv()
        if step in (0, 2):
            for lo, hi in halves:
                pz_send[step // 2, lo:hi] = third_sum(step, lo, hi).astype(bf16)
            zcopy["p", step] = send(pz_send.at[step // 2], pz_recv.at[step // 2], z0dev)
        elif step == 1:
            zcopy["p", 0].wait_recv()
            for lo, hi in halves:
                pw_send[lo:hi] = (third_sum(step, lo, hi) + pz_recv[0, lo:hi].astype(f32)).astype(bf16)
            zcopy["p", 1] = send(pw_send, pw_recv, z1dev)
        else:
            zcopy["p", 1].wait_recv()
            zcopy["p", 2].wait_recv()
            for lo, hi in halves:
                out[lo:hi] = third_sum(step, lo, hi) + pz_recv[1, lo:hi].astype(f32) + pw_recv[lo:hi].astype(f32)

    def c_across():
        zcopy["c", 0].wait_recv()
        cw_send[...] = (ck[0] + cz_recv[0].astype(f32)).astype(bf16)
        zcopy["c", 1] = send(cw_send, cw_recv, z1dev)

    def c_sum(lo, hi):
        return ck[1, lo:hi] + cz_recv[1, lo:hi].astype(f32) + cw_recv[lo:hi].astype(f32)

    def c_x():
        zcopy["c", 2].wait_recv()
        zcopy["c", 1].wait_recv()
        cx_send[...] = c_sum(0, 2 * nc).astype(bf16)
        zcopy["cx"] = send(cx_send, cx_recv, xdev)
        ckx[...] = c_sum(2 * nc, 4 * nc)

    def c_y():
        zcopy["cx"].wait_recv()
        cy_send[...] = (ckx[0:nc] + cx_recv[0:nc].astype(f32)).astype(bf16)
        zcopy["cy"] = send(cy_send, cy_recv, ydev)
        ckx[nc:2 * nc] = ckx[nc:2 * nc] + cx_recv[nc:2 * nc].astype(f32)

    build(0)
    for step in range(4):
        product(step, 0, c_send.at[step], bf16)
        if step == 0:
            pl.semaphore_wait(barrier, 5)
        stage1[step, "c"] = send(c_send.at[step], c_recv.at[step], core)
        product(step, 1, own, f32)
        if step == 2:
            c_across()
        if step < 3:
            build(step + 1)
        first(step)
        if step >= 2:
            second(step - 2)
    third(0)
    second(2)
    c_x()
    second(3)
    third(1)
    c_y()
    third(2)
    third(3)
    zcopy["cy"].wait_recv()
    out[nab:shard] = ckx[nc:2 * nc] + cy_recv[...].astype(f32)
    aux_lanes = gamma.shape[1]
    gamma[...] = out[0:shard, 0:aux_lanes] * scale
    out[shard:] = jnp.zeros((out.shape[0] - shard, lanes), f32)
    turned[...] = out[:, aux_lanes:].T * scale
    strip = virt.shape[0]
    virt[...] = turned[pl.ds(pl.multiple_of(z0 * (turned.shape[0] - strip), 8), strip), 0:shard]
    for copy in started:
        copy.wait_send()


COPIES = 4 + 8 + 8 + 2 + 1 + 2 + 1 + 2


def by_kernel(integrals, amplitudes, pno_density, pno_coef, pao_blocks, aux_slice, aux_offset):
    n_pair = lax.axis_size("pair")
    n_aux = lax.axis_size("aux")
    pairs, rows, rank = pno_coef.shape
    block = rows // pao_blocks.shape[1]
    ao_count = NBLK * block
    shard = ao_count // n_pair
    na, nb, nc = group_rows(shard)
    nab = na + nb
    aux_lanes = ABPO * block
    lanes = aux_lanes + 2 * block
    width = pairs * rank
    scale = 1.0 / math.sqrt(pairs * n_pair)
    vmem = pl.BlockSpec(memory_space=pltpu.VMEM)
    smem = pl.BlockSpec(memory_space=pltpu.SMEM)

    def half(*dims):
        return pltpu.VMEM(dims + (lanes,), jnp.bfloat16)

    def full(*dims):
        return pltpu.VMEM(dims + (lanes,), jnp.float32)

    gamma, virt = pl.pallas_call(
        functools.partial(kernel, scale),
        out_shape=[
            jax.ShapeDtypeStruct((shard, aux_lanes), jnp.float32),
            jax.ShapeDtypeStruct((ao_count // n_aux, shard), jnp.float32),
        ],
        in_specs=[vmem] * 4 + [smem] * 3,
        out_specs=[vmem] * 2,
        scratch_shapes=[
            full(TILE),
            pltpu.VMEM((rows, width), jnp.bfloat16),
            pltpu.VMEM((width, rows), jnp.bfloat16),
            pltpu.VMEM((width, rows), jnp.bfloat16),
            pltpu.VMEM((2, SUB, width), jnp.int32),
            pltpu.VMEM((8 * shard, width), jnp.bfloat16),
            pltpu.VMEM((2, width, lanes), jnp.bfloat16),
            full(4 * shard),
            half(4, 4 * shard), half(4, 4 * shard),
            half(4, 2 * na), half(4, 2 * na), half(4, na), half(4, na),
            half(4, 2 * nb), half(4, 2 * nb), half(4, nb), half(4, nb),
            full(4, 2 * nab), full(4, nab),
            half(2, 4 * nc), half(2, 4 * nc), half(4 * nc), half(4 * nc), full(2, 4 * nc),
            half(2, nab), half(2, nab), half(nab), half(nab),
            half(2 * nc), half(2 * nc), half(nc), half(nc), full(2 * nc),
            pltpu.VMEM((2 * block, TILE), jnp.float32),
            pltpu.SemaphoreType.DMA((COPIES,)),
            pltpu.SemaphoreType.DMA((COPIES,)),
        ],
        compiler_params=pltpu.CompilerParams(
            collective_id=0, has_side_effects=True, vmem_limit_bytes=60 * 1024 * 1024),
    )(integrals.swapaxes(1, 2), amplitudes, pno_density, pno_coef.swapaxes(1, 2),
      pao_blocks.T, aux_slice.T, aux_offset.T)
    return gamma.T, virt


def on_device(*args):
    pairs, rows, rank = args[3].shape
    fits = lax.axis_size("pair") == 8 and lax.axis_size("aux") == 4 and pairs % 2 == 0 and 2 * rank == TILE
    fits = fits and rows == 2 * TILE and args[0].shape[1] == 2 * TILE
    return by_kernel(*args) if fits else by_collectives(*args)


def solution(mesh):
    in_specs = (
        P(("pair", "aux"), None, None),
        P(("pair", "aux"), None, None),
        P(("pair", "aux"), None, None),
        P(("pair", "aux"), None, None),
        P(("pair", "aux"), None),
        P(("pair", "aux"), None),
        P(("pair", "aux"), None),
    )
    out_specs = (P("aux", "pair"), P("aux", "pair"))
    return jax.shard_map(
        on_device, mesh=mesh, in_specs=in_specs, out_specs=out_specs, check_vma=False
    )
```

profile of v0, /device:TPU:0, one launch (start us, length us, event | category | flops | bytes accessed | tf_op | source)
XLA Modules:
  0.0 39.1 jit_solution(7375388818288062781)
XLA Ops:
  0.6 36.2 %shard_map.86 = (f32[96,512]{1,0:T(8,128)}, f32[192,96]{1,0:T(8,128)}) custom-call(bf16[16,64,256]{2,1,0:T(8,128)(2,1)} %bitcast.6, bf16[16,64,64]{2,1,0:T(8,128)(2,1)} %amps.1, bf16[16,64,64]{2,1,0:T(8,128)(2,1)} %dens.1, bf16[16,64,256]{2,1,0:T(8,128)(2,1)} %bitcast.7, s32[2,16]{1,0:T(2,128)} %bitcast.9, s32[2,16]{1,0:T(2,128)} %bitcast.10, s32[2,16]{1,0:T(2,128)} %bitcast.11), custom_call_target="tpu_custom_call" | custom-call | tf_op jit(solution)/shard_map/pallas_call | solution.py:388
  36.8 0.0 copy-start
  36.8 1.6 %copy.11 = f32[512,96]{0,1:T(8,128)} copy(f32[512,96]{0,1:T(8,128)} %bitcast.8) | data formatting | bytes 393216
  38.5 0.0 copy-done
  38.5 0.6 %copy.12 = f32[192,96]{1,0:T(8,128)} copy(f32[192,96]{1,0:T(8,128)S(1)} %copy-done) | data formatting | bytes 147456
Async XLA Ops:
  36.8 1.7 %copy-start = (f32[192,96]{1,0:T(8,128)S(1)}, f32[192,96]{1,0:T(8,128)}, u32[]{:S(2)}) copy-start(f32[192,96]{1,0:T(8,128)} %get-tuple-element.9) | copy-start | bytes 221188
where the time goes:
time: 39.3 us; the launch traced here: 39.1 us
  Pallas kernels  36.2 us (92%)
  local copies, waits for them, and re-layouts  2.29 us (6%)
  between operations  0.65 us (2%)
    pallas_call x1, Pallas kernels, by_kernel(): pl.pallas_call(functools.partial(kernel, scale), out_shape=[jax.ShapeDtyp...  36.2 us
    unnamed x4, local copies, waits for them, and re-layouts  2.29 us

commit v1 on v0

v1 whole, which is shorter than its diff:
```python
import functools
import math

import jax
import jax.numpy as jnp
from jax import lax
from jax.experimental import pallas as pl
from jax.experimental.pallas import tpu as pltpu
from jax.sharding import PartitionSpec as P

NBLK = 6
ABPO = 4
MESH = pl.DeviceIdType.MESH
TILE = 128
SUB = 16


def by_collectives(integrals, amplitudes, pno_density, pno_coef, pao_blocks, aux_slice, aux_offset):
    n_pair = lax.axis_size("pair")
    n_aux = lax.axis_size("aux")
    pair_count, domain_rows, pno_rank = pno_coef.shape
    aux_dom = aux_slice.shape[1]
    pao_dom = pao_blocks.shape[1]
    pao_block = domain_rows // pao_dom
    aux_block = integrals.shape[1] // aux_dom
    ao_count = NBLK * pao_block
    capacity = max(2, 2 * pair_count * aux_dom // n_aux)
    out_scale = 1.0 / math.sqrt(pair_count * n_pair)
    slot_count = pair_count * aux_dom
    three_index = jnp.einsum(
        "pqr,prs->pqs", integrals, amplitudes, preferred_element_type=jnp.float32
    ).astype(jnp.bfloat16)
    owners = aux_slice.reshape(slot_count)
    owner_hot = (owners[:, None] == jnp.arange(n_aux, dtype=jnp.int32)[None, :]).astype(jnp.int32)
    before = jnp.cumsum(owner_hot, 0) - owner_hot
    slot_rank = jnp.sum(before * owner_hot, 1)
    target = owners * capacity + slot_rank
    routing = jnp.arange(n_aux * capacity, dtype=jnp.int32)[:, None] == target[None, :]
    labels = (
        jnp.concatenate(
            [aux_offset.reshape(slot_count, 1), jnp.repeat(pao_blocks, aux_dom, axis=0)], 1
        )
        + 1
    )
    label_buffer = (jnp.dot(routing.astype(jnp.int32), labels) - 1).reshape(
        n_aux, capacity, 1 + pao_dom
    )
    routing_bf = routing.astype(jnp.bfloat16)
    index_flat = three_index.reshape(slot_count, aux_block * pno_rank)
    index_buffer = jnp.dot(routing_bf, index_flat, preferred_element_type=jnp.float32).astype(
        jnp.bfloat16
    )
    index_buffer = index_buffer.reshape(n_aux, capacity, aux_block, pno_rank)
    pair_routing = (
        routing.reshape(n_aux * capacity, pair_count, aux_dom).sum(-1).astype(jnp.bfloat16)
    )
    coef_flat = pno_coef.reshape(pair_count, domain_rows * pno_rank)
    coef_buffer = jnp.dot(pair_routing, coef_flat, preferred_element_type=jnp.float32).astype(
        jnp.bfloat16
    )
    coef_buffer = coef_buffer.reshape(n_aux, capacity, domain_rows, pno_rank)
    index_part = lax.all_to_all(index_buffer, "aux", split_axis=0, concat_axis=0, tiled=True)
    coef_part = lax.all_to_all(coef_buffer, "aux", split_axis=0, concat_axis=0, tiled=True)
    label_part = lax.all_to_all(label_buffer, "aux", split_axis=0, concat_axis=0, tiled=True)
    back = jnp.einsum(
        "ncxr,ncyr->ncxy", index_part, coef_part, preferred_element_type=jnp.float32
    ).astype(jnp.bfloat16)
    got_labels = label_part
    received_count = n_aux * capacity
    pieces = back.reshape(received_count, aux_block, pao_dom, pao_block)
    got_labels = got_labels.reshape(received_count, 1 + pao_dom)
    offset_hot = got_labels[:, 0:1] == jnp.arange(ABPO, dtype=jnp.int32)[None, :]
    column_hot = got_labels[:, 1:, None] == jnp.arange(NBLK, dtype=jnp.int32)[None, None, :]
    placement = (offset_hot[:, None, :, None] & column_hot[:, :, None, :]).astype(jnp.bfloat16)
    gamma_part = jnp.einsum(
        "sxhy,shok->oxky", pieces, placement, preferred_element_type=jnp.float32
    )
    gamma_part = gamma_part.reshape(ABPO * aux_block, ao_count)
    aux_density = lax.psum_scatter(gamma_part, "pair", scatter_dimension=1, tiled=True) * out_scale
    weighted = jnp.einsum(
        "pyr,prs->pys", pno_coef, pno_density, preferred_element_type=jnp.float32
    ).astype(jnp.bfloat16)
    block_hot = (pao_blocks[:, :, None] == jnp.arange(NBLK, dtype=jnp.int32)[None, None, :]).astype(
        jnp.bfloat16
    )
    weighted_rows = jnp.einsum(
        "pak,paxr->kxpr",
        block_hot,
        weighted.reshape(pair_count, pao_dom, pao_block, pno_rank),
        preferred_element_type=jnp.float32,
    ).astype(jnp.bfloat16)
    weighted_rows = weighted_rows.reshape(ao_count, pair_count * pno_rank)
    coef_rows = jnp.einsum(
        "pak,paxr->kxpr",
        block_hot,
        pno_coef.reshape(pair_count, pao_dom, pao_block, pno_rank),
        preferred_element_type=jnp.float32,
    ).astype(jnp.bfloat16)
    coef_rows = coef_rows.reshape(ao_count, pair_count * pno_rank)
    virt_part = lax.dot_general(
        weighted_rows, coef_rows, (((1,), (1,)), ((), ())), preferred_element_type=jnp.float32
    )
    row_owned = lax.psum_scatter(virt_part, "aux", scatter_dimension=0, tiled=True)
    virtual_density = lax.psum_scatter(row_owned, "pair", scatter_dimension=1, tiled=True)
    return (aux_density, virtual_density * out_scale)


TILES = (("virt", 0, 0), ("virt", 0, 1), ("virt", 0, 2), ("aux", "far", 0), ("aux", "far", 1),
         ("aux", "early", 0), ("aux", "late", 0), ("aux", "early", 1), ("aux", "late", 1), ("aux", "own", 0), ("aux", "own", 1))
WIDE = 2 * TILE
RECVS = 3 * len(TILES) + 9
SENDS = 6


def kernel(scale, ints_in, amps_in, dens_in, coef_in, pao_in, aux_in, off_in, gamma, virt,
           ints, amps, dens, coef, pao, aux, off, labels, coef2, tri2, wei2, lhs, rhs, own, c_send, c_recv,
           s1_send, s1_recv, s2_send, s2_recv, keep1, keep2,
           p_send, p_recv, f_send, f_recv, v_send, v_recv, v_sum, flat, turned, load_sems, send_sems, recv_sems):
    pairs, rank, rows = coef.shape
    couples = pairs // 2
    shard = gamma.shape[0]
    part = shard // 2
    half_rows = 4 * shard
    f32, bf16 = jnp.float32, jnp.bfloat16
    p = lax.axis_index("pair")
    z = lax.axis_index("aux")
    c, x, y = p % 2, (p // 2) % 2, p // 4
    z0, z1 = z % 2, z // 2
    core = (p + 1 - 2 * c, z)
    xdev = (p + 2 - 4 * x, z)
    ydev = (p + 4 - 8 * y, z)
    flips = (z, z + 1 - 2 * z0, z + 2 - 4 * z1, 3 - z)
    at_end = 1 - (z0 + z1) % 2
    early, late = 1 + at_end, 2 - at_end
    flip_of = {"own": 0, "far": 3, "early": early, "late": late}
    owner_of = {"own": z, "far": flips[3], "early": flips[1] + at_end * (flips[2] - flips[1]),
                "late": flips[2] + at_end * (flips[1] - flips[2])}

    loads = [
        pltpu.make_async_copy(src, dst, load_sems.at[n])
        for n, (src, dst) in enumerate((
            (pao_in, pao), (coef_in, coef), (dens_in, dens), (amps_in, amps), (ints_in, ints), (aux_in, aux), (off_in, off)))
    ]
    for load in loads:
        load.start()

    barrier = pltpu.get_barrier_semaphore()
    for dev in (core, xdev, ydev) + tuple((p, flips[n]) for n in (1, 2, 3)):
        pl.semaphore_signal(barrier, inc=1, device_id=dev, device_id_type=MESH)

    def send(src, dst, family, slot, dev):
        pltpu.make_async_remote_copy(
            src_ref=src, dst_ref=dst, send_sem=send_sems.at[family], recv_sem=recv_sems.at[slot],
            device_id=dev, device_id_type=MESH).start()

    def arrived(ref, slot):
        pltpu.make_async_copy(ref, ref, recv_sems.at[slot]).wait()

    zero = jnp.zeros((rank, rank), bf16)

    def mixed(ref, q, both):
        diag = jnp.concatenate(
            [jnp.concatenate([ref[2 * q], zero], 1), jnp.concatenate([zero, ref[2 * q + 1]], 1)], 0)
        return lax.dot_general(
            diag, both, (((0,), (0,)), ((), ())), preferred_element_type=f32).astype(bf16)

    def keep(dst, q, value):
        dst[q * TILE:(q + 1) * TILE, :] = value

    with jax.named_scope("turn"):
        loads[1].wait()
        for q in range(couples):
            at = slice(q * TILE, (q + 1) * TILE)
            coef2[:, at] = coef[2 * q:2 * q + 2].reshape(2 * rank, rows).T

    def splat(flag, count):
        return jnp.full((count, TILE), jnp.where(flag, 1.0, 0.0), f32).astype(bf16)

    low = jnp.where(lax.broadcasted_iota(jnp.int32, (SUB, TILE), 1) < rank, 1.0, 0.0).astype(bf16)
    high = jnp.where(lax.broadcasted_iota(jnp.int32, (SUB, TILE), 1) < rank, 0.0, 1.0).astype(bf16)

    with jax.named_scope("lhs"):
        loads[0].wait()

        def place_of(s):
            bits = s % 2, (s // 2) % 2, s // 4
            same = [me if bit else 1 - me for bit, me in zip(bits, (c, x, y))]
            return same[0] * half_rows + (same[1] * 2 + same[2]) * part, same[0] * half_rows + 2 * shard + (same[2] * 2 + same[1]) * part

        places = [place_of(s) for s in range(2 * half_rows // shard)]
        for b in range(NBLK):
            for q in range(couples):
                at = slice(q * TILE, (q + 1) * TILE)
                m0, m1 = [splat(pao[h, 2 * q] == b, SUB) * low + splat(pao[h, 2 * q + 1] == b, SUB) * high for h in range(2)]
                for r in range(0, TILE, SUB):
                    s, inner = divmod(b * TILE + r, shard)
                    group, inner = divmod(inner, part)
                    dst = pl.ds(pl.multiple_of(places[s][group] + inner, SUB), SUB)
                    lhs[dst, at] = coef2[r:r + SUB, at] * m0 + coef2[TILE + r:TILE + r + SUB, at] * m1

    with jax.named_scope("mix"):
        loads[2].wait()
        for q in range(couples):
            keep(wei2, q, mixed(dens, q, coef[2 * q:2 * q + 2].reshape(2 * rank, rows)))

    def mix_integrals():
        for n in range(3, 7):
            loads[n].wait()
        for h in range(2):
            for n in range(pairs):
                labels[h * pairs + n] = aux[h, n] * ABPO + off[h, n]
        for q in range(couples):
            keep(tri2, q, mixed(amps, q, ints[2 * q:2 * q + 2].reshape(2 * rank, rows)))

    def build(t):
        kind, role, piece = TILES[t]

        for n in range(pairs):
            at = slice(n * rank, (n + 1) * rank)
            if kind == "aux":
                src, first = tri2, owner_of[role] * ABPO + 2 * piece
                names = [labels[h * pairs + n] for h in range(2)]
            else:
                src, first = wei2, 2 * piece
                names = [pao[h, n] for h in range(2)]
            low_part, high_part = src[at, 0:TILE], src[at, TILE:2 * TILE]
            for j in range(2):
                rhs[t % 2, at, j * TILE:(j + 1) * TILE] = (
                    low_part * splat(names[0] == first + j, rank) + high_part * splat(names[1] == first + j, rank))

    def product(t, half):
        return lax.dot_general(
            lhs[half * half_rows:(half + 1) * half_rows, :], rhs[t % 2], (((1,), (0,)), ((), ())),
            preferred_element_type=f32)

    count = len(TILES)
    stage1, stage2, to_owner, to_far, to_virt = count, 2 * count, 3 * count, 3 * count + 6, 3 * count + 7

    def make(t):
        with jax.named_scope(f"make{t}"):
            c_send[t] = product(t, 0).astype(bf16)
            if t == 0:
                pl.semaphore_wait(barrier, 6)
                send(c_send.at[t], c_recv.at[t], 0, t, core)
            own[t % 2] = product(t, 1)
            if t + 1 < count and t != 2:
                build(t + 1)
        if t:
            send(c_send.at[t], c_recv.at[t], 0, t, core)

    def first(t):
        with jax.named_scope(f"first{t}"):
            arrived(c_recv.at[t], t)

            def summed(lo):
                return own[t % 2, lo:lo + shard] + c_recv[t, lo:lo + shard].astype(f32)

            s1_send[t, 0:shard] = summed(0).astype(bf16)
            at = pl.ds(0, shard)
            send(s1_send.at[t, at], s1_recv.at[t, at], 1, stage1 + t, xdev)
            s1_send[t, shard:2 * shard] = summed(2 * shard).astype(bf16)
            at = pl.ds(shard, shard)
            send(s1_send.at[t, at], s1_recv.at[t, at], 1, stage1 + t, ydev)
            keep1[t, 0:shard] = summed(shard)
            keep1[t, shard:2 * shard] = summed(3 * shard)

    def second(t):
        with jax.named_scope(f"second{t}"):
            arrived(s1_recv.at[t], stage1 + t)
            for lo, dev in ((0, ydev), (part, xdev)):
                near = slice(2 * lo, 2 * lo + part)
                s2_send[t, lo:lo + part] = (keep1[t, near] + s1_recv[t, near].astype(f32)).astype(bf16)
                at = pl.ds(lo, part)
                send(s2_send.at[t, at], s2_recv.at[t, at], 2, stage2 + t, dev)
            for lo in (0, part):
                rest = slice(2 * lo + part, 2 * lo + shard)
                keep2[t, lo:lo + part] = keep1[t, rest] + s1_recv[t, rest].astype(f32)

    def third(t):
        kind, role, piece = TILES[t]
        with jax.named_scope(f"third{t}"):
            arrived(s2_recv.at[t], stage2 + t)
            if role == "early":
                arrived(p_recv.at[4 + piece], to_owner + 4 + piece)
            if role == "own":
                arrived(p_recv.at[piece], to_owner + piece)
                arrived(p_recv.at[2 + piece], to_owner + 2 + piece)
            total = keep2[t] + s2_recv[t].astype(f32)
            if kind == "virt":
                for j in range(2):
                    v_sum[2 * piece + j] = total[:, j * TILE:(j + 1) * TILE]
                if piece == 2:
                    f_send[...] = v_sum[blocks_of(flips[3])].astype(bf16)
                    send(f_send, f_recv, 4, to_far, (p, flips[1]))
            elif role == "own":
                gamma[:, piece * WIDE:(piece + 1) * WIDE] = (
                    total + p_recv[piece].astype(f32) + p_recv[2 + piece].astype(f32)) * scale
            else:
                flip = flip_of[role]
                if role != "far":
                    total = total + p_recv[4 + piece].astype(f32) * (flip - 1).astype(f32)
                n = 2 * flip - 2 + piece
                p_send[n] = total.astype(bf16)
                dev = flips[1] if role == "far" else owner_of[role]
                send(p_send.at[n], p_recv.at[n], 3, to_owner + n, (p, dev))

    def blocks_of(owner):
        return pl.ds(3 * (owner // 2) + owner % 2, 2)

    def virt_across():
        with jax.named_scope("virt_across"):
            arrived(f_recv, to_far)
            v_send[0] = v_sum[blocks_of(flips[1])].astype(bf16)
            v_send[1] = (v_sum[blocks_of(flips[2])] + f_recv[...].astype(f32)).astype(bf16)
            for role in ("early", "late"):
                n = flip_of[role] - 1
                send(v_send.at[n], v_recv.at[n], 5, to_virt + n, (p, owner_of[role]))

    def virt_out():
        with jax.named_scope("virt_out"):
            for n in range(2):
                arrived(v_recv.at[n], to_virt + n)
            total = v_sum[blocks_of(z)] + v_recv[0].astype(f32) + v_recv[1].astype(f32)
            strip = virt.shape[0]
            for j in range(2):
                flat[0:shard, j * TILE:(j + 1) * TILE] = total[j] * scale
            flat[shard:] = jnp.zeros((TILE - shard, WIDE), f32)
            turned[...] = flat[...].T
            virt[...] = turned[pl.ds(pl.multiple_of(z0 * (WIDE - strip), 8), strip), 0:shard]

    with jax.named_scope("pipeline"):
        build(0)
        for t in range(count + 5):
            if t < count:
                make(t)
            if t == 2:
                with jax.named_scope("mix_integrals"):
                    mix_integrals()
                    build(3)
            if 0 <= t - 1 < count:
                first(t - 1)
            if 0 <= t - 3 < count:
                second(t - 3)
            if 0 <= t - 5 < count:
                third(t - 5)
            if t == 9:
                virt_across()
            if t == 13:
                virt_out()
    for family, ref in enumerate((c_send, s1_send, s2_send, p_send, f_send, v_send)):
        pltpu.make_async_copy(ref, ref, send_sems.at[family]).wait()


def put_out(gamma, virt, gamma_out, virt_out, sems):
    copies = [pltpu.make_async_copy(gamma, gamma_out, sems.at[0]), pltpu.make_async_copy(virt, virt_out, sems.at[1])]
    for copy in copies:
        copy.start()
    for copy in copies:
        copy.wait()


def by_kernel(integrals, amplitudes, pno_density, pno_coef, pao_blocks, aux_slice, aux_offset):
    n_pair = lax.axis_size("pair")
    n_aux = lax.axis_size("aux")
    pairs, rows, rank = pno_coef.shape
    block = rows // pao_blocks.shape[1]
    ao_count = NBLK * block
    shard = ao_count // n_pair
    part = shard // 2
    width = pairs * rank
    count = len(TILES)
    scale = 1.0 / math.sqrt(pairs * n_pair)
    hbm = pl.BlockSpec(memory_space=pltpu.HBM)
    vmem = pl.BlockSpec(memory_space=pltpu.VMEM)

    def half(*dims):
        return pltpu.VMEM(dims, jnp.bfloat16)

    def full(*dims):
        return pltpu.VMEM(dims, jnp.float32)

    operands = (integrals.swapaxes(1, 2), amplitudes, pno_density, pno_coef.swapaxes(1, 2),
                pao_blocks.T, aux_slice.T, aux_offset.T)
    operands = tuple(pltpu.with_memory_space_constraint(a, pltpu.HBM) for a in operands)
    gamma, virt = pl.pallas_call(
        functools.partial(kernel, scale),
        out_shape=[
            jax.ShapeDtypeStruct((shard, ABPO * block), jnp.float32),
            jax.ShapeDtypeStruct((ao_count // n_aux, shard), jnp.float32),
        ],
        in_specs=[hbm] * 7,
        out_specs=[vmem] * 2,
        scratch_shapes=[half(*a.shape) for a in operands[:4]] + [pltpu.SMEM(a.shape, jnp.int32) for a in operands[4:]] + [
            pltpu.SMEM((2 * pairs,), jnp.int32),
            half(rows, width), half(width, rows), half(width, rows),
            half(8 * shard, width), half(2, width, WIDE), full(2, 4 * shard, WIDE),
            half(count, 4 * shard, WIDE), half(count, 4 * shard, WIDE)]
        + [half(count, 2 * shard, WIDE)] * 2 + [half(count, shard, WIDE)] * 2 + [
            full(count, 2 * shard, WIDE), full(count, shard, WIDE),
            half(6, shard, WIDE), half(6, shard, WIDE),
            half(2, shard, TILE), half(2, shard, TILE), half(2, 2, shard, TILE), half(2, 2, shard, TILE), full(NBLK, shard, TILE),
            full(TILE, WIDE), full(WIDE, TILE),
            pltpu.SemaphoreType.DMA((7,)),
            pltpu.SemaphoreType.DMA((SENDS,)),
            pltpu.SemaphoreType.DMA((RECVS,)),
        ],
        compiler_params=pltpu.CompilerParams(
            collective_id=0, has_side_effects=True, vmem_limit_bytes=36 * 1024 * 1024),
    )(*operands)
    gamma, virt = [pltpu.with_memory_space_constraint(a, pltpu.VMEM) for a in (gamma, virt)]
    gamma, virt = pl.pallas_call(
        put_out,
        out_shape=[jax.ShapeDtypeStruct(a.shape, a.dtype) for a in (gamma, virt)],
        in_specs=[vmem] * 2,
        out_specs=[hbm] * 2,
        scratch_shapes=[pltpu.SemaphoreType.DMA((2,))],
    )(gamma, virt)
    return gamma.T, virt


def on_device(*args):
    pairs, rows, rank = args[3].shape
    fits = lax.axis_size("pair") == 8 and lax.axis_size("aux") == 4 and pairs % 2 == 0 and 2 * rank == TILE
    fits = fits and rows == 2 * TILE and args[0].shape[1] == 2 * TILE
    return by_kernel(*args) if fits else by_collectives(*args)


def solution(mesh):
    in_specs = (
        P(("pair", "aux"), None, None),
        P(("pair", "aux"), None, None),
        P(("pair", "aux"), None, None),
        P(("pair", "aux"), None, None),
        P(("pair", "aux"), None),
        P(("pair", "aux"), None),
        P(("pair", "aux"), None),
    )
    out_specs = (P("aux", "pair"), P("aux", "pair"))
    return jax.shard_map(
        on_device, mesh=mesh, in_specs=in_specs, out_specs=out_specs, check_vma=False
    )
```

time: 39.3 us -> 32.5 us (0.83)
  Pallas kernels: 36.2 us -> 31.7 us
  local copies, waits for them, and re-layouts: 2.29 us -> 0 us
    pallas_call x1, Pallas kernels: 36.2 us -> 31 us  [by_kernel(): pl.pallas_call(functools.partial(kernel, scale), out_shape=[jax.ShapeDtyp...]
    unnamed x4 -> x0, local copies, waits for them, and re-layouts: 2.29 us -> none
    pallas_call x0 -> x1, Pallas kernels: none -> 0.72 us  [by_kernel(): pl.pallas_call(put_out, out_shape=[jax.ShapeDtypeStruct(a.shape, a.dtype)...]
where the time goes in v1:
time: 32.5 us; the launch traced here: 32.3 us
  Pallas kernels  31.7 us (98%)
  between operations  0.64 us (2%)
    pallas_call x1, Pallas kernels, by_kernel(): pl.pallas_call(functools.partial(kernel, scale), out_shape=[jax.ShapeDtyp...  31 us
    pallas_call x1, Pallas kernels, by_kernel(): pl.pallas_call(put_out, out_shape=[jax.ShapeDtypeStruct(a.shape, a.dtype)...  0.72 us

profile of v1, /device:TPU:0, one launch (start us, length us, event | category | flops | bytes accessed | tf_op | source)
XLA Modules:
  0.0 32.3 jit_solution(10733574897568618847)
XLA Ops:
  0.6 31.0 %shard_map.86 = (f32[96,512]{1,0:T(8,128)S(1)}, f32[192,96]{1,0:T(8,128)S(1)}) custom-call(bf16[16,64,256]{2,1,0:T(8,128)(2,1)} %bitcast.6, bf16[16,64,64]{2,1,0:T(8,128)(2,1)} %amps_in.1, bf16[16,64,64]{2,1,0:T(8,128)(2,1)} %dens_in.1, bf16[16,64,256]{2,1,0:T(8,128)(2,1)} %bitcast.7, s32[2,16]{1,0:T(2,128)} %bitcast.8, s32[2,16]{1,0:T(2,128)} %bitcast.9, ...), custom_call_target="tpu_custom_call" | custom-call | tf_op jit(solution)/shard_map/pallas_call | solution.py:385
  31.6 0.7 %shard_map.87 = (f32[96,512]{1,0:T(8,128)}, f32[192,96]{1,0:T(8,128)}) custom-call(f32[96,512]{1,0:T(8,128)S(1)} %get-tuple-element.6.gamma, f32[192,96]{1,0:T(8,128)S(1)} %get-tuple-element.7.virt), custom_call_target="tpu_custom_call" | custom-call | tf_op jit(solution)/shard_map/pallas_call | solution.py:411

commit v2 on v1

--- a/solution.py
+++ b/solution.py
@@ -130,7 +130,7 @@
     xdev = (p + 2 - 4 * x, z)
     ydev = (p + 4 - 8 * y, z)
     flips = (z, z + 1 - 2 * z0, z + 2 - 4 * z1, 3 - z)
-    at_end = 1 - (z0 + z1) % 2
+    at_end = 1 - z0 * (1 - z1)
     early, late = 1 + at_end, 2 - at_end
     flip_of = {"own": 0, "far": 3, "early": early, "late": late}
     owner_of = {"own": z, "far": flips[3], "early": flips[1] + at_end * (flips[2] - flips[1]),

time: 32.5 us -> 31 us (0.954)
  Pallas kernels: 31.7 us -> 30.2 us
    pallas_call x1, Pallas kernels: 31 us -> 29.5 us  [by_kernel(): pl.pallas_call(functools.partial(kernel, scale), out_shape=[jax.ShapeDtyp...]
where the time goes in v2:
time: 31 us; the launch traced here: 30.9 us
  Pallas kernels  30.2 us (97%)
  between operations  0.64 us (2%)
    pallas_call x1, Pallas kernels, by_kernel(): pl.pallas_call(functools.partial(kernel, scale), out_shape=[jax.ShapeDtyp...  29.5 us
    pallas_call x1, Pallas kernels, by_kernel(): pl.pallas_call(put_out, out_shape=[jax.ShapeDtypeStruct(a.shape, a.dtype)...  0.72 us

profile of v2, /device:TPU:0, one launch (start us, length us, event | category | flops | bytes accessed | tf_op | source)
XLA Modules:
  0.0 30.9 jit_solution(14821530673822908492)
XLA Ops:
  0.6 29.5 %shard_map.86 = (f32[96,512]{1,0:T(8,128)S(1)}, f32[192,96]{1,0:T(8,128)S(1)}) custom-call(bf16[16,64,256]{2,1,0:T(8,128)(2,1)} %bitcast.6, bf16[16,64,64]{2,1,0:T(8,128)(2,1)} %amps_in.1, bf16[16,64,64]{2,1,0:T(8,128)(2,1)} %dens_in.1, bf16[16,64,256]{2,1,0:T(8,128)(2,1)} %bitcast.7, s32[2,16]{1,0:T(2,128)} %bitcast.8, s32[2,16]{1,0:T(2,128)} %bitcast.9, ...), custom_call_target="tpu_custom_call" | custom-call | tf_op jit(solution)/shard_map/pallas_call | solution.py:385
  30.2 0.7 %shard_map.87 = (f32[96,512]{1,0:T(8,128)}, f32[192,96]{1,0:T(8,128)}) custom-call(f32[96,512]{1,0:T(8,128)S(1)} %get-tuple-element.6.gamma, f32[192,96]{1,0:T(8,128)S(1)} %get-tuple-element.7.virt), custom_call_target="tpu_custom_call" | custom-call | tf_op jit(solution)/shard_map/pallas_call | solution.py:411

commit v3 on v2

--- a/solution.py
+++ b/solution.py
@@ -333,12 +333,12 @@
         for t in range(count + 5):
             if t < count:
                 make(t)
+            if 0 <= t - 1 < count:
+                first(t - 1)
             if t == 2:
                 with jax.named_scope("mix_integrals"):
                     mix_integrals()
                     build(3)
-            if 0 <= t - 1 < count:
-                first(t - 1)
             if 0 <= t - 3 < count:
                 second(t - 3)
             if 0 <= t - 5 < count:

time: 31 us -> 30.8 us (level)
  no operation moved by 1% of the time
where the time goes in v3:
time: 30.8 us; the launch traced here: 30.7 us
  Pallas kernels  30 us (97%)
  between operations  0.64 us (2%)
    pallas_call x1, Pallas kernels, by_kernel(): pl.pallas_call(functools.partial(kernel, scale), out_shape=[jax.ShapeDtyp...  29.3 us
    pallas_call x1, Pallas kernels, by_kernel(): pl.pallas_call(put_out, out_shape=[jax.ShapeDtypeStruct(a.shape, a.dtype)...  0.72 us

profile of v3, /device:TPU:0, one launch (start us, length us, event | category | flops | bytes accessed | tf_op | source)
XLA Modules:
  0.0 30.7 jit_solution(6053021754705191014)
XLA Ops:
  0.6 29.3 %shard_map.86 = (f32[96,512]{1,0:T(8,128)S(1)}, f32[192,96]{1,0:T(8,128)S(1)}) custom-call(bf16[16,64,256]{2,1,0:T(8,128)(2,1)} %bitcast.6, bf16[16,64,64]{2,1,0:T(8,128)(2,1)} %amps_in.1, bf16[16,64,64]{2,1,0:T(8,128)(2,1)} %dens_in.1, bf16[16,64,256]{2,1,0:T(8,128)(2,1)} %bitcast.7, s32[2,16]{1,0:T(2,128)} %bitcast.8, s32[2,16]{1,0:T(2,128)} %bitcast.9, ...), custom_call_target="tpu_custom_call" | custom-call | tf_op jit(solution)/shard_map/pallas_call | solution.py:385
  29.9 0.7 %shard_map.87 = (f32[96,512]{1,0:T(8,128)}, f32[192,96]{1,0:T(8,128)}) custom-call(f32[96,512]{1,0:T(8,128)S(1)} %get-tuple-element.6.gamma, f32[192,96]{1,0:T(8,128)S(1)} %get-tuple-element.7.virt), custom_call_target="tpu_custom_call" | custom-call | tf_op jit(solution)/shard_map/pallas_call | solution.py:411
